TPU v7x, 32 devices: a whole 2x2x4 slice. The times are simulated.
32 devices in a mesh: lon: 8 (over y, x, core), dp: 4 (over z).
Axes of the slice: x: 2, y: 2, z: 4, core: 2. Of those that a mesh axis runs over, the one named last changes fastest.
Arguments:
- inputs: bfloat16 [4, 32, 384, 256], P('dp', None, 'lon'), may hold values from -6 to 6
- pre_act: bfloat16 [4, 32, 384, 256], P('dp', None, 'lon'), may hold values from -6 to 6
- cotangent: bfloat16 [4, 32, 384, 256], P('dp', None, 'lon'), may hold values from -6 to 6
- first_weight: bfloat16 [2304, 256], replicated, may hold values from -0.125 to 0.125
- second_weight: bfloat16 [2304, 256], replicated, may hold values from -0.125 to 0.125
Outputs:
- input_gradient_array: bfloat16 [4, 32, 384, 256], P('dp', None, 'lon')
- first_weight_gradient: float32 [589824], P(('lon', 'dp'))
- second_weight_gradient: float32 [589824], P(('lon', 'dp'))
All inputs are finite; a program needn't handle non-finite values.
Results may differ from a plain program's by a relative error of at most 0.0049.
Values may be sent and summed in bfloat16 or wider, within the bound.
A program may use at most 64 MiB of HBM per device.

v0:
```python
import functools

import jax
import jax.numpy as jnp
from jax import lax
from jax.experimental import pallas as pl
from jax.experimental.pallas import tpu as pltpu
from jax.sharding import PartitionSpec as P

FIRST_SPREAD = 12
SECOND_SPREAD = 18
MESH = pl.DeviceIdType.MESH
F32 = jnp.float32
BF16 = jnp.bfloat16
LANE_SLOT = (0, 2, 1)


def row_span(rows, dilation, r):
    if r == 0:
        return 0, rows - dilation, dilation
    if r == 1:
        return 0, rows, 0
    return dilation, rows, 0


def dot_nt(a, b):
    return lax.dot_general(a, b, (((1,), (1,)), ((), ())), preferred_element_type=F32)


def dot_tn(a, b):
    return lax.dot_general(a, b, (((0,), (0,)), ((), ())), preferred_element_type=F32)


def flat(v):
    return v.reshape(-1, v.shape[-1])


def kernel(nl, nd, scatter, norm, *refs):
    inp, pre, cot, w1, w2 = refs[:5]
    ig_out, g1_out, g2_out = refs[5:8]
    (cot_v, pre_v, inp_v, lg_v, ig_v, w1_v, w2_v, side2, side1, acc) = refs[8:18]
    (in_sem, w1_sem, w2_sem, out_sem) = refs[18:22]
    (s2_lo, s2_hi, r2_lo, r2_hi, s1_lo, s1_hi, r1_lo, r1_hi, hs_sem, hr_sem) = refs[22:32]
    if scatter:
        (dw1, dw2, ps1, ps2, pr1, pr2, as1, as2, ar1, ar2) = refs[32:42]
        (zs1, zs2, zr1, zr2, p_ssem, p_rsem, a_ssem, a_rsem, z_ssem, z_rsem) = refs[42:52]
    else:
        dw1, dw2 = g1_out, g2_out

    rows, cols, ch = cot_v.shape
    me_l, me_d = lax.axis_index("lon"), lax.axis_index("dp")
    left, right = lax.rem(me_l + nl - 1, nl), lax.rem(me_l + 1, nl)
    half = nl // 2
    slots = half * nd
    core = lax.rem(me_l, 2)

    my_chip = me_l // 2

    def plane_device(t):
        return (2 * lax.rem(my_chip + t, half) + core, me_d)

    def depth_device(u):
        return (me_l, lax.rem(me_d + u, nd))

    load_cot = pltpu.make_async_copy(cot.at[0], cot_v, in_sem.at[0])
    load_pre = pltpu.make_async_copy(pre.at[0], pre_v, in_sem.at[1])
    load_inp = pltpu.make_async_copy(inp.at[0], inp_v, in_sem.at[2])

    def weight_loads(w, w_v, sem):
        return [
            pltpu.make_async_copy(
                w.at[pl.ds(k * ch, ch)],
                w_v.at[k // 3, :, pl.ds(LANE_SLOT.index(k % 3) * ch, ch)],
                sem.at[k],
            )
            for k in range(9)
        ]

    load_w2 = weight_loads(w2, w2_v, w2_sem)
    load_w1 = weight_loads(w1, w1_v, w1_sem)
    load_cot.start()
    for c in load_w2:
        c.start()
    load_pre.start()
    load_inp.start()
    for c in load_w1:
        c.start()

    barrier = pltpu.get_barrier_semaphore()
    for other in (left, right):
        pl.semaphore_signal(barrier, inc=1, device_id=(other, me_d), device_id_type=MESH)
    greeted = 2
    if scatter:
        for t in range(1, half):
            pl.semaphore_signal(barrier, inc=1, device_id=plane_device(t), device_id_type=MESH)
        for u in range(1, nd):
            pl.semaphore_signal(barrier, inc=1, device_id=depth_device(u), device_id_type=MESH)
        greeted += half - 1 + nd - 1

    def halo_copies(lo, hi, from_right, from_left, base):
        return (
            pltpu.make_async_remote_copy(
                src_ref=lo, dst_ref=from_right, send_sem=hs_sem.at[base],
                recv_sem=hr_sem.at[base], device_id=(left, me_d), device_id_type=MESH,
            ),
            pltpu.make_async_remote_copy(
                src_ref=hi, dst_ref=from_left, send_sem=hs_sem.at[base + 1],
                recv_sem=hr_sem.at[base + 1], device_id=(right, me_d), device_id_type=MESH,
            ),
        )

    def pack(src, lo, hi, d):
        for p in range(rows):
            lo[p * d : (p + 1) * d, :] = src[p, 0:d, :]
            hi[p * d : (p + 1) * d, :] = src[p, cols - d : cols, :]

    def side_inner(src, side, d):
        side[:, 0 : cols - d, 0:ch] = src[:, d:cols, :]
        side[:, d:cols, ch : 2 * ch] = src[:, 0 : cols - d, :]

    def side_edges(side, from_right, from_left, d):
        side[:, cols - d : cols, 0:ch] = from_right[...].reshape(rows, d, ch)
        side[:, 0:d, ch : 2 * ch] = from_left[...].reshape(rows, d, ch)

    def input_terms(src, lanes, w_v, wl, d, fresh):
        for r in (1, 0, 2):
            lo, hi, first = row_span(rows, d, r)
            term = dot_nt(
                flat(src[first : first + hi - lo, :, 0:lanes]), w_v[r, :, wl : wl + lanes]
            )
            if fresh and r == 1:
                acc[...] = term
            else:
                acc[lo * cols : hi * cols, :] += term

    def weight_terms(x, src, lanes, dw, taps, d):
        for r in range(3):
            lo, hi, first = row_span(rows, d, r)
            term = dot_tn(flat(x[lo:hi]), flat(src[first : first + hi - lo, :, 0:lanes]))
            for at, c in enumerate(taps):
                k = 3 * r + c
                value = term[:, at * ch : (at + 1) * ch]
                dw[k * ch : (k + 1) * ch, :] = value if scatter else value * norm

    if scatter:
        depth = dw1.shape[0] // (nl * nd)
        plane_order = (*range(1, half), 0)

        def chunk_rows(slot, parity):
            l, d = 2 * (slot // nd) + parity, lax.rem(slot, nd)
            return pl.ds(pl.multiple_of((l * nd + d) * depth, 8), depth)

        def pair_copy(ps, pr, at, t):
            part = pl.ds(lax.rem(my_chip + t, half) * nd, nd)
            return pltpu.make_async_remote_copy(
                src_ref=ps.at[part], dst_ref=pr.at[part],
                send_sem=p_ssem.at[at, t], recv_sem=p_rsem.at[at, t],
                device_id=(me_l + 1 - 2 * core, me_d), device_id_type=MESH,
            )

        def pair_send(dw, ps, pr, at):
            for t in plane_order:
                for d in range(nd):
                    s = lax.rem(my_chip + t, half) * nd + d
                    v = dw[chunk_rows(s, 1 - core), :].astype(BF16)
                    ps[s, 0:depth, :] = v[:, : ch // 2]
                    ps[s, depth : 2 * depth, :] = v[:, ch // 2 :]
                pair_copy(ps, pr, at, t).start()

        def chip_sum(dw, pr, s):
            v = dw[chunk_rows(s, core), :]
            return (
                v[:, : ch // 2] + pr[s, 0:depth, :].astype(F32),
                v[:, ch // 2 :] + pr[s, depth : 2 * depth, :].astype(F32),
            )

        def plane_copy(a_s, a_r, at, t):
            chip = lax.rem(my_chip + t, half)
            return pltpu.make_async_remote_copy(
                src_ref=a_s.at[pl.ds(chip * nd, nd)], dst_ref=a_r.at[pl.ds(t * nd, nd)],
                send_sem=a_ssem.at[at, t], recv_sem=a_rsem.at[at, t],
                device_id=plane_device(t), device_id_type=MESH,
            )

        def depth_copy(z_s, z_r, at, u):
            return pltpu.make_async_remote_copy(
                src_ref=z_s.at[lax.rem(me_d + u, nd)], dst_ref=z_r.at[u],
                send_sem=z_ssem.at[at, u], recv_sem=z_rsem.at[at, u],
                device_id=depth_device(u), device_id_type=MESH,
            )

        def spread(dw, ps, pr, a_s, a_r, at):
            for t in plane_order:
                pair_copy(ps, pr, at, t).wait()
                if t == 0:
                    continue
                for d in range(nd):
                    s = lax.rem(my_chip + t, half) * nd + d
                    lo, hi = chip_sum(dw, pr, s)
                    a_s[s, 0:depth, :] = lo.astype(BF16)
                    a_s[s, depth : 2 * depth, :] = hi.astype(BF16)
                plane_copy(a_s, a_r, at, t).start()

        def plane_sum(dw, pr, a_r, d):
            lo, hi = chip_sum(dw, pr, my_chip * nd + d)
            for t in range(1, half):
                lo += a_r[t * nd + d, 0:depth, :].astype(F32)
                hi += a_r[t * nd + d, depth : 2 * depth, :].astype(F32)
            return lo, hi

        def across(dw, pr, a_s, a_r, z_s, z_r, at):
            for t in range(1, half):
                plane_copy(a_s, a_r, at, t).wait()

            for u in range(1, nd):
                d = lax.rem(me_d + u, nd)
                lo, hi = plane_sum(dw, pr, a_r, d)
                z_s[d, 0:depth, :] = lo.astype(BF16)
                z_s[d, depth : 2 * depth, :] = hi.astype(BF16)
                depth_copy(z_s, z_r, at, u).start()

        def gather_sum(dw, pr, a_r, z_s, z_r, at, out):
            lo, hi = plane_sum(dw, pr, a_r, me_d)
            for u in range(1, nd):
                depth_copy(z_s, z_r, at, u).wait()
                lo += z_r[u, 0:depth, :].astype(F32)
                hi += z_r[u, depth : 2 * depth, :].astype(F32)
            out[pl.ds(0, depth, stride=2), :] = lo * norm
            out[pl.ds(1, depth, stride=2), :] = hi * norm

    load_cot.wait()
    pack(cot_v, s2_lo, s2_hi, SECOND_SPREAD)
    pl.semaphore_wait(barrier, greeted)
    halo2 = halo_copies(s2_lo, s2_hi, r2_lo, r2_hi, 0)
    for c in halo2:
        c.start()
    side_inner(cot_v, side2, SECOND_SPREAD)
    for c in load_w2:
        c.wait()
    input_terms(cot_v, ch, w2_v, 2 * ch, SECOND_SPREAD, True)
    load_pre.wait()
    zero = jnp.zeros((), BF16)
    pre_v[...] = jnp.maximum(pre_v[...], zero)
    weight_terms(pre_v, cot_v, ch, dw2, (1,), SECOND_SPREAD)
    for c in halo2:
        c.wait()
    side_edges(side2, r2_lo, r2_hi, SECOND_SPREAD)
    input_terms(side2, 2 * ch, w2_v, 0, SECOND_SPREAD, False)
    grad = jnp.where(flat(pre_v[...]) > 0, acc[...], F32(0.0)).astype(BF16)
    lg_v[...] = grad.reshape(rows, cols, ch)
    pack(lg_v, s1_lo, s1_hi, FIRST_SPREAD)
    halo1 = halo_copies(s1_lo, s1_hi, r1_lo, r1_hi, 2)
    for c in halo1:
        c.start()
    weight_terms(pre_v, side2, 2 * ch, dw2, (0, 2), SECOND_SPREAD)
    if scatter:
        pair_send(dw2, ps2, pr2, 0)

    load_inp.wait()
    side_inner(lg_v, side1, FIRST_SPREAD)
    weight_terms(inp_v, lg_v, ch, dw1, (1,), FIRST_SPREAD)
    if scatter:
        spread(dw2, ps2, pr2, as2, ar2, 0)
    for c in halo1:
        c.wait()
    side_edges(side1, r1_lo, r1_hi, FIRST_SPREAD)
    weight_terms(inp_v, side1, 2 * ch, dw1, (0, 2), FIRST_SPREAD)
    if scatter:
        pair_send(dw1, ps1, pr1, 1)
    for c in load_w1:
        c.wait()
    input_terms(lg_v, ch, w1_v, 2 * ch, FIRST_SPREAD, True)
    if scatter:
        spread(dw1, ps1, pr1, as1, ar1, 1)
        across(dw2, pr2, as2, ar2, zs2, zr2, 0)
    input_terms(side1, 2 * ch, w1_v, 0, FIRST_SPREAD, False)
    ig_v[...] = acc[...].astype(BF16).reshape(rows, cols, ch)
    store = pltpu.make_async_copy(ig_v, ig_out.at[0], out_sem)
    store.start()
    if scatter:
        across(dw1, pr1, as1, ar1, zs1, zr1, 1)
        gather_sum(dw2, pr2, ar2, zs2, zr2, 0, g2_out)
        gather_sum(dw1, pr1, ar1, zs1, zr1, 1, g1_out)
    store.wait()


def local(nl, nd, inputs, pre_act, cotangent, first_weight, second_weight):
    _, rows, cols, ch = inputs.shape
    taps_rows = first_weight.shape[0]
    norm = float(rows * cols * nl * inputs.shape[0] * nd) ** -0.5
    devices = nl * nd
    depth = taps_rows // devices
    scatter = nl % 2 == 0 and taps_rows % devices == 0 and depth % 8 == 0
    slots = devices // 2
    vm = pltpu.VMEM
    dma = pltpu.SemaphoreType.DMA
    field = vm((rows, cols, ch), BF16)
    edge2 = vm((rows * SECOND_SPREAD, ch), BF16)
    edge1 = vm((rows * FIRST_SPREAD, ch), BF16)
    weights = vm((3, ch, 3 * ch), BF16)
    side = vm((rows, cols, 2 * ch), BF16)
    scratch = [field] * 5 + [weights] * 2 + [side] * 2 + [vm((rows * cols, ch), F32)]
    scratch += [dma((3,)), dma((9,)), dma((9,)), dma]
    scratch += [edge2] * 4 + [edge1] * 4 + [dma((4,)), dma((4,))]
    if scatter:
        pieces = vm((slots, 2 * depth, ch // 2), BF16)
        scratch += [vm((taps_rows, ch), F32)] * 2 + [pieces] * 8
        scratch += [vm((nd, 2 * depth, ch // 2), BF16)] * 4
        scratch += [dma((2, nl // 2))] * 4 + [dma((2, nd))] * 2
        grad_shape = (2 * depth, ch // 2)
    else:
        grad_shape = (taps_rows, ch)
    any_spec = pl.BlockSpec(memory_space=pl.ANY)
    vmem_spec = pl.BlockSpec(memory_space=pltpu.VMEM)
    ig, g1, g2 = pl.pallas_call(
        functools.partial(kernel, nl, nd, scatter, norm),
        out_shape=(
            jax.ShapeDtypeStruct(inputs.shape, BF16),
            jax.ShapeDtypeStruct(grad_shape, F32),
            jax.ShapeDtypeStruct(grad_shape, F32),
        ),
        in_specs=[any_spec] * 5,
        out_specs=(any_spec, vmem_spec, vmem_spec),
        scratch_shapes=scratch,
        compiler_params=pltpu.CompilerParams(
            collective_id=0, has_side_effects=True, vmem_limit_bytes=62 * 1024 * 1024
        ),
        name="conv_backward",
    )(inputs, pre_act, cotangent, first_weight, second_weight)
    g1, g2 = g1.reshape(-1), g2.reshape(-1)
    if not scatter:
        g1, g2 = (lax.psum_scatter(g, "lon", scatter_dimension=0, tiled=True) for g in (g1, g2))
        g1, g2 = (lax.psum_scatter(g, "dp", scatter_dimension=0, tiled=True) for g in (g1, g2))
    return ig, g1, g2


def solution(mesh):
    in_specs = (
        P("dp", None, "lon", None),
        P("dp", None, "lon", None),
        P("dp", None, "lon", None),
        P(),
        P(),
    )
    out_specs = (P("dp", None, "lon", None), P(("lon", "dp")), P(("lon", "dp")))
    step = functools.partial(local, mesh.shape["lon"], mesh.shape["dp"])
    return jax.shard_map(step, mesh=mesh, in_specs=in_specs, out_specs=out_specs, check_vma=False)
```

profile of v0, /device:TPU:0, one launch (start us, length us, event | category | flops | bytes accessed | tf_op | source)
XLA Modules:
  0.0 43.6 jit_solution(1988447406553250573)
XLA Ops:
  0.6 39.5 %conv_backward.1 = (bf16[1,32,48,256]{3,2,1,0:T(8,128)(2,1)}, f32[144,128]{1,0:T(8,128)}, f32[144,128]{1,0:T(8,128)}) custom-call(bf16[1,32,48,256]{3,2,1,0:T(8,128)(2,1)} %refs_0_.1, bf16[1,32,48,256]{3,2,1,0:T(8,128)(2,1)} %refs_1_.1, bf16[1,32,48,256]{3,2,1,0:T(8,128)(2,1)} %refs_2_.1, bf16[2304,256]{1,0:T(8,128)(2,1)} %refs_3_.1, bf16[2304,256]{1,0:T(8,128)(2,1)} %refs_4_.1), custom_call_target="tpu_custom_call" | custom-call | tf_op jit(solution)/shard_map/conv_backward/pallas_call | solution.py:315
  40.2 0.0 copy-start.1
  40.2 0.0 copy-start
  40.2 2.1 %copy.11 = bf16[1,32,48,256]{3,2,1,0:T(8,128)(2,1)} copy(bf16[1,32,48,256]{3,2,1,0:T(8,128)(2,1)} %get-tuple-element.12) | data formatting | bytes 1572864
  42.3 0.0 copy-done.1
  42.3 0.6 %copy.12 = f32[18432]{0:T(1024)} copy(f32[18432]{0:T(1024)S(1)} %bitcast.3) | data formatting | bytes 147456
  42.9 0.0 copy-done
  42.9 0.6 %copy.13 = f32[18432]{0:T(1024)} copy(f32[18432]{0:T(1024)S(1)} %bitcast.2) | data formatting | bytes 147456
Async XLA Ops:
  40.2 2.1 %copy-start.1 = (f32[144,128]{1,0:T(8,128)S(1)}, f32[144,128]{1,0:T(8,128)}, u32[]{:S(2)}) copy-start(f32[144,128]{1,0:T(8,128)} %get-tuple-element.7) | copy-start | bytes 221188
  40.2 2.8 %copy-start = (f32[144,128]{1,0:T(8,128)S(1)}, f32[144,128]{1,0:T(8,128)}, u32[]{:S(2)}) copy-start(f32[144,128]{1,0:T(8,128)} %get-tuple-element.8) | copy-start | bytes 221188
where the time goes:
time: 43.7 us; the launch traced here: 43.6 us
  Pallas kernels  39.5 us (90%)
  local copies, waits for them, and re-layouts  3.38 us (8%)
  between operations  0.66 us (2%)
    pallas_call x1, Pallas kernels, local(): pl.pallas_call(functools.partial(kernel, nl, nd, scatter, norm), out_shap...  39.5 us
    unnamed x7, local copies, waits for them, and re-layouts  3.38 us

commit v1 on v0

--- a/solution.py
+++ b/solution.py
@@ -38,12 +38,12 @@
 def kernel(nl, nd, scatter, norm, *refs):
     inp, pre, cot, w1, w2 = refs[:5]
     ig_out, g1_out, g2_out = refs[5:8]
-    (cot_v, pre_v, inp_v, lg_v, ig_v, w1_v, w2_v, side2, side1, acc) = refs[8:18]
-    (in_sem, w1_sem, w2_sem, out_sem) = refs[18:22]
-    (s2_lo, s2_hi, r2_lo, r2_hi, s1_lo, s1_hi, r1_lo, r1_hi, hs_sem, hr_sem) = refs[22:32]
-    if scatter:
-        (dw1, dw2, ps1, ps2, pr1, pr2, as1, as2, ar1, ar2) = refs[32:42]
-        (zs1, zs2, zr1, zr2, p_ssem, p_rsem, a_ssem, a_rsem, z_ssem, z_rsem) = refs[42:52]
+    (cot_v, pre_v, inp_v, lg_v, w1_v, w2_v, side2, side1, acc) = refs[8:17]
+    (in_sem, w1_sem, w2_sem) = refs[17:20]
+    (s2_lo, s2_hi, r2_lo, r2_hi, s1_lo, s1_hi, r1_lo, r1_hi, hs_sem, hr_sem) = refs[20:30]
+    if scatter:
+        (dw1, dw2, ps1, ps2, pr1, pr2, as1, as2, ar1, ar2) = refs[30:40]
+        (zs1, zs2, zr1, zr2, p_ssem, p_rsem, a_ssem, a_rsem, z_ssem, z_rsem) = refs[40:50]
     else:
         dw1, dw2 = g1_out, g2_out
 
@@ -274,14 +274,35 @@
         spread(dw1, ps1, pr1, as1, ar1, 1)
         across(dw2, pr2, as2, ar2, zs2, zr2, 0)
     input_terms(side1, 2 * ch, w1_v, 0, FIRST_SPREAD, False)
-    ig_v[...] = acc[...].astype(BF16).reshape(rows, cols, ch)
-    store = pltpu.make_async_copy(ig_v, ig_out.at[0], out_sem)
-    store.start()
+    ig_out[0] = acc[...].astype(BF16).reshape(rows, cols, ch)
     if scatter:
         across(dw1, pr1, as1, ar1, zs1, zr1, 1)
         gather_sum(dw2, pr2, ar2, zs2, zr2, 0, g2_out)
         gather_sum(dw1, pr1, ar1, zs1, zr1, 1, g1_out)
-    store.wait()
+
+
+def emit_kernel(*refs):
+    count = len(refs) // 2
+    copies = [
+        pltpu.make_async_copy(refs[i], refs[count + i], refs[-1].at[i]) for i in range(count)
+    ]
+    for c in copies:
+        c.start()
+    for c in copies:
+        c.wait()
+
+
+def emit(*values):
+    any_spec = pl.BlockSpec(memory_space=pl.ANY)
+    vmem_spec = pl.BlockSpec(memory_space=pltpu.VMEM)
+    return pl.pallas_call(
+        emit_kernel,
+        out_shape=[jax.ShapeDtypeStruct(v.shape, v.dtype) for v in values],
+        in_specs=[vmem_spec] * len(values),
+        out_specs=[any_spec] * len(values),
+        scratch_shapes=[pltpu.SemaphoreType.DMA((len(values),))],
+        name="emit",
+    )(*(pltpu.with_memory_space_constraint(v, pltpu.VMEM) for v in values))
 
 
 def local(nl, nd, inputs, pre_act, cotangent, first_weight, second_weight):
@@ -299,8 +320,8 @@
     edge1 = vm((rows * FIRST_SPREAD, ch), BF16)
     weights = vm((3, ch, 3 * ch), BF16)
     side = vm((rows, cols, 2 * ch), BF16)
-    scratch = [field] * 5 + [weights] * 2 + [side] * 2 + [vm((rows * cols, ch), F32)]
-    scratch += [dma((3,)), dma((9,)), dma((9,)), dma]
+    scratch = [field] * 4 + [weights] * 2 + [side] * 2 + [vm((rows * cols, ch), F32)]
+    scratch += [dma((3,)), dma((9,)), dma((9,))]
     scratch += [edge2] * 4 + [edge1] * 4 + [dma((4,)), dma((4,))]
     if scatter:
         pieces = vm((slots, 2 * depth, ch // 2), BF16)
@@ -312,21 +333,24 @@
         grad_shape = (taps_rows, ch)
     any_spec = pl.BlockSpec(memory_space=pl.ANY)
     vmem_spec = pl.BlockSpec(memory_space=pltpu.VMEM)
+    place = vm if scatter else jax.ShapeDtypeStruct
     ig, g1, g2 = pl.pallas_call(
         functools.partial(kernel, nl, nd, scatter, norm),
         out_shape=(
-            jax.ShapeDtypeStruct(inputs.shape, BF16),
-            jax.ShapeDtypeStruct(grad_shape, F32),
-            jax.ShapeDtypeStruct(grad_shape, F32),
+            place(inputs.shape, BF16),
+            place(grad_shape, F32),
+            place(grad_shape, F32),
         ),
         in_specs=[any_spec] * 5,
-        out_specs=(any_spec, vmem_spec, vmem_spec),
+        out_specs=(vmem_spec, vmem_spec, vmem_spec),
         scratch_shapes=scratch,
         compiler_params=pltpu.CompilerParams(
-            collective_id=0, has_side_effects=True, vmem_limit_bytes=62 * 1024 * 1024
+            collective_id=0, has_side_effects=True, vmem_limit_bytes=48 * 1024 * 1024
         ),
         name="conv_backward",
     )(inputs, pre_act, cotangent, first_weight, second_weight)
+    if scatter:
+        ig, g1, g2 = emit(ig, g1, g2)
     g1, g2 = g1.reshape(-1), g2.reshape(-1)
     if not scatter:
         g1, g2 = (lax.psum_scatter(g, "lon", scatter_dimension=0, tiled=True) for g in (g1, g2))

time: 43.7 us -> 47 us (1.076)
  local copies, waits for them, and re-layouts: 3.38 us -> 5.93 us
  Pallas kernels: 39.5 us -> 40.1 us
    unnamed x7 -> x10, local copies, waits for them, and re-layouts: 3.38 us -> 5.93 us
    pallas_call x0 -> x1, Pallas kernels: none -> 0.94 us  [emit(): pl.pallas_call(emit_kernel, out_shape=[jax.ShapeDtypeStruct(v.shape, v.dt...]
where the time goes in v1:
time: 47 us; the launch traced here: 46.6 us
  Pallas kernels  40.1 us (85%)
  local copies, waits for them, and re-layouts  5.93 us (13%)
  between operations  0.65 us (1%)
    pallas_call x1, Pallas kernels, local(): pl.pallas_call(functools.partial(kernel, nl, nd, scatter, norm), out_shap...  39.1 us
    unnamed x10, local copies, waits for them, and re-layouts  5.93 us
    pallas_call x1, Pallas kernels, emit(): pl.pallas_call(emit_kernel, out_shape=[jax.ShapeDtypeStruct(v.shape, v.dt...  0.94 us

profile of v1, /device:TPU:0, one launch (start us, length us, event | category | flops | bytes accessed | tf_op | source)
XLA Modules:
  0.0 46.6 jit_solution(986438840628250053)
XLA Ops:
  0.6 0.0 copy-start
  0.6 1.3 %copy-done = bf16[2304,256]{1,0:T(8,128)(2,1)S(1)} copy-done((bf16[2304,256]{1,0:T(8,128)(2,1)S(1)}, bf16[2304,256]{1,0:T(8,128)(2,1)}, u32[]{:S(2)}) %copy-start) | copy-done | bytes 1179672
  1.9 0.0 copy-start.1
  1.9 1.3 %copy-done.1 = bf16[2304,256]{1,0:T(8,128)(2,1)S(1)} copy-done((bf16[2304,256]{1,0:T(8,128)(2,1)S(1)}, bf16[2304,256]{1,0:T(8,128)(2,1)}, u32[]{:S(2)}) %copy-start.1) | copy-done | bytes 1179672
  3.2 0.0 copy-start.2
  3.2 1.1 %copy-done.2 = bf16[1,32,48,256]{3,2,1,0:T(8,128)(2,1)S(1)} copy-done((bf16[1,32,48,256]{3,2,1,0:T(8,128)(2,1)S(1)}, bf16[1,32,48,256]{3,2,1,0:T(8,128)(2,1)}, u32[]{:S(2)}) %copy-start.2) | copy-done | bytes 786456
  4.3 0.0 copy-start.3
  4.3 1.1 %copy-done.3 = bf16[1,32,48,256]{3,2,1,0:T(8,128)(2,1)S(1)} copy-done((bf16[1,32,48,256]{3,2,1,0:T(8,128)(2,1)S(1)}, bf16[1,32,48,256]{3,2,1,0:T(8,128)(2,1)}, u32[]{:S(2)}) %copy-start.3) | copy-done | bytes 786456
  5.4 0.0 copy-start.4
  5.4 1.1 %copy-done.4 = bf16[1,32,48,256]{3,2,1,0:T(8,128)(2,1)S(1)} copy-done((bf16[1,32,48,256]{3,2,1,0:T(8,128)(2,1)S(1)}, bf16[1,32,48,256]{3,2,1,0:T(8,128)(2,1)}, u32[]{:S(2)}) %copy-start.4) | copy-done | bytes 786456
  6.6 39.1 %conv_backward.1 = (bf16[1,32,48,256]{3,2,1,0:T(8,128)(2,1)S(1)}, f32[144,128]{1,0:T(8,128)S(1)}, f32[144,128]{1,0:T(8,128)S(1)}) custom-call(bf16[1,32,48,256]{3,2,1,0:T(8,128)(2,1)S(1)} %copy-done.2, bf16[1,32,48,256]{3,2,1,0:T(8,128)(2,1)S(1)} %copy-done.3, bf16[1,32,48,256]{3,2,1,0:T(8,128)(2,1)S(1)} %copy-done.4, bf16[2304,256]{1,0:T(8,128)(2,1)S(1)} %copy-done, ...), custom_call_target="tpu_custom_call" | custom-call | tf_op jit(solution)/shard_map/conv_backward/pallas_call | solution.py:337
  45.7 0.9 %emit.1 = (bf16[1,32,48,256]{3,2,1,0:T(8,128)(2,1)}, f32[144,128]{1,0:T(8,128)}, f32[144,128]{1,0:T(8,128)}) custom-call(bf16[1,32,48,256]{3,2,1,0:T(8,128)(2,1)S(1)} %get-tuple-element.9.refs_0_, f32[144,128]{1,0:T(8,128)S(1)} %get-tuple-element.10.refs_1_, f32[144,128]{1,0:T(8,128)S(1)} %get-tuple-element.11.refs_2_), custom_call_target="tpu_custom_call" | custom-call | tf_op jit(solution)/shard_map/emit/pallas_call | solution.py:298
Async XLA Ops:
  0.6 1.3 %copy-start = (bf16[2304,256]{1,0:T(8,128)(2,1)S(1)}, bf16[2304,256]{1,0:T(8,128)(2,1)}, u32[]{:S(2)}) copy-start(bf16[2304,256]{1,0:T(8,128)(2,1)} %refs_3_.1) | copy-start | bytes 3538948
  1.9 1.3 %copy-start.1 = (bf16[2304,256]{1,0:T(8,128)(2,1)S(1)}, bf16[2304,256]{1,0:T(8,128)(2,1)}, u32[]{:S(2)}) copy-start(bf16[2304,256]{1,0:T(8,128)(2,1)} %refs_4_.1) | copy-start | bytes 3538948
  3.2 1.1 %copy-start.2 = (bf16[1,32,48,256]{3,2,1,0:T(8,128)(2,1)S(1)}, bf16[1,32,48,256]{3,2,1,0:T(8,128)(2,1)}, u32[]{:S(2)}) copy-start(bf16[1,32,48,256]{3,2,1,0:T(8,128)(2,1)} %refs_0_.1) | copy-start | bytes 2359300
  4.3 1.1 %copy-start.3 = (bf16[1,32,48,256]{3,2,1,0:T(8,128)(2,1)S(1)}, bf16[1,32,48,256]{3,2,1,0:T(8,128)(2,1)}, u32[]{:S(2)}) copy-start(bf16[1,32,48,256]{3,2,1,0:T(8,128)(2,1)} %refs_1_.1) | copy-start | bytes 2359300
  5.4 1.1 %copy-start.4 = (bf16[1,32,48,256]{3,2,1,0:T(8,128)(2,1)S(1)}, bf16[1,32,48,256]{3,2,1,0:T(8,128)(2,1)}, u32[]{:S(2)}) copy-start(bf16[1,32,48,256]{3,2,1,0:T(8,128)(2,1)} %refs_2_.1) | copy-start | bytes 2359300

commit v2 on v1

--- a/solution.py
+++ b/solution.py
@@ -345,7 +345,7 @@
         out_specs=(vmem_spec, vmem_spec, vmem_spec),
         scratch_shapes=scratch,
         compiler_params=pltpu.CompilerParams(
-            collective_id=0, has_side_effects=True, vmem_limit_bytes=48 * 1024 * 1024
+            collective_id=0, has_side_effects=True, vmem_limit_bytes=62 * 1024 * 1024
         ),
         name="conv_backward",
     )(inputs, pre_act, cotangent, first_weight, second_weight)

time: 47 us -> 40.6 us (0.86)
  local copies, waits for them, and re-layouts: 5.93 us -> 0 us
    unnamed x10 -> x0, local copies, waits for them, and re-layouts: 5.93 us -> none
where the time goes in v2:
time: 40.6 us; the launch traced here: 40.4 us
  Pallas kernels  39.8 us (98%)
  between operations  0.64 us (2%)
    pallas_call x1, Pallas kernels, local(): pl.pallas_call(functools.partial(kernel, nl, nd, scatter, norm), out_shap...  38.9 us
    pallas_call x1, Pallas kernels, emit(): pl.pallas_call(emit_kernel, out_shape=[jax.ShapeDtypeStruct(v.shape, v.dt...  0.94 us

profile of v2, /device:TPU:0, one launch (start us, length us, event | category | flops | bytes accessed | tf_op | source)
XLA Modules:
  0.0 40.4 jit_solution(17145580178236533440)
XLA Ops:
  0.6 38.9 %conv_backward.1 = (bf16[1,32,48,256]{3,2,1,0:T(8,128)(2,1)S(1)}, f32[144,128]{1,0:T(8,128)S(1)}, f32[144,128]{1,0:T(8,128)S(1)}) custom-call(bf16[1,32,48,256]{3,2,1,0:T(8,128)(2,1)} %refs_0_.1, bf16[1,32,48,256]{3,2,1,0:T(8,128)(2,1)} %refs_1_.1, bf16[1,32,48,256]{3,2,1,0:T(8,128)(2,1)} %refs_2_.1, bf16[2304,256]{1,0:T(8,128)(2,1)} %refs_3_.1, ...), custom_call_target="tpu_custom_call" | custom-call | tf_op jit(solution)/shard_map/conv_backward/pallas_call | solution.py:337
  39.5 0.9 %emit.1 = (bf16[1,32,48,256]{3,2,1,0:T(8,128)(2,1)}, f32[144,128]{1,0:T(8,128)}, f32[144,128]{1,0:T(8,128)}) custom-call(bf16[1,32,48,256]{3,2,1,0:T(8,128)(2,1)S(1)} %get-tuple-element.9.refs_0_, f32[144,128]{1,0:T(8,128)S(1)} %get-tuple-element.10.refs_1_, f32[144,128]{1,0:T(8,128)S(1)} %get-tuple-element.11.refs_2_), custom_call_target="tpu_custom_call" | custom-call | tf_op jit(solution)/shard_map/emit/pallas_call | solution.py:298

commit v3 on v2

v3 whole, which is shorter than its diff:
```python
import functools

import jax
import jax.numpy as jnp
from jax import lax
from jax.experimental import pallas as pl
from jax.experimental.pallas import tpu as pltpu
from jax.sharding import PartitionSpec as P

FIRST_SPREAD = 12
SECOND_SPREAD = 18
MESH = pl.DeviceIdType.MESH
F32 = jnp.float32
BF16 = jnp.bfloat16
LANE_SLOT = (0, 2, 1)


def row_span(rows, dilation, r):
    if r == 0:
        return 0, rows - dilation, dilation
    if r == 1:
        return 0, rows, 0
    return dilation, rows, 0


def row_blocks(rows, dilation):
    cuts = sorted({0, dilation, rows - dilation, rows})
    blocks = []
    for lo, hi in zip(cuts, cuts[1:]):
        taps = []
        for r in range(3):
            start, stop, first = row_span(rows, dilation, r)
            if start <= lo and hi <= stop:
                taps.append((r, first + lo - start))
        blocks.append((lo, hi, taps))
    return blocks


def dot_nt(a, b):
    return lax.dot_general(a, b, (((1,), (1,)), ((), ())), preferred_element_type=F32)


def dot_tn(a, b):
    return lax.dot_general(a, b, (((0,), (0,)), ((), ())), preferred_element_type=F32)


def flat(v):
    return v.reshape(-1, v.shape[-1])


def kernel(nl, nd, scatter, norm, *refs):
    refs = list(refs)

    def take(count):
        taken = refs[:count]
        del refs[:count]
        return taken

    inp, pre, cot, w1, w2 = take(5)
    ig_out, g1_out, g2_out = take(3)
    pre_v, inp_v, w1_v, w2_v, side2, side1, acc = take(7)
    cot_e, pre_e, inp_e, acc_e = take(4)
    in_sem, w1_sem, w2_sem = take(3)
    sa, ra, sb, rb, sc, rc, hs_sem, hr_sem = take(8)
    if scatter:
        dw1, dw2 = take(2)
        sums = [take(10) for _ in range(2)]
        p_ssem, p_rsem, a_ssem, a_rsem, b_ssem, b_rsem, c_ssem, c_rsem, d_ssem, d_rsem = take(10)
    else:
        dw1, dw2 = g1_out, g2_out

    rows, cols, ch = pre_v.shape
    first_d, second_d = FIRST_SPREAD, SECOND_SPREAD
    rest = second_d - first_d
    me_l, me_d = lax.axis_index("lon"), lax.axis_index("dp")
    left, right = lax.rem(me_l + nl - 1, nl), lax.rem(me_l + 1, nl)
    half = nl // 2
    core = lax.rem(me_l, 2)
    my_chip = me_l // 2
    cot_v = side2.at[:, :, pl.ds(2 * ch, ch)]
    lg_v = side1.at[:, :, pl.ds(2 * ch, ch)]
    section = pl.when(me_l >= 0)

    def plane_device(t):
        return (2 * lax.rem(my_chip + t, half) + core, me_d)

    def depth_device(u):
        return (me_l, lax.rem(me_d + u, nd))

    load_cot = pltpu.make_async_copy(cot.at[0], cot_v, in_sem.at[0])
    load_pre = pltpu.make_async_copy(pre.at[0], pre_v, in_sem.at[1])
    load_inp = pltpu.make_async_copy(inp.at[0], inp_v, in_sem.at[2])

    def weight_loads(w, w_v, sem):
        return [
            pltpu.make_async_copy(
                w.at[pl.ds(k * ch, ch)],
                w_v.at[k // 3, :, pl.ds(LANE_SLOT.index(k % 3) * ch, ch)],
                sem.at[k],
            )
            for k in range(9)
        ]

    load_w2 = weight_loads(w2, w2_v, w2_sem)
    load_w1 = weight_loads(w1, w1_v, w1_sem)
    load_cot.start()

    barrier = pltpu.get_barrier_semaphore()
    for other in (left, right):
        pl.semaphore_signal(barrier, inc=1, device_id=(other, me_d), device_id_type=MESH)
    greeted = 2
    if scatter:
        for t in range(1, half):
            pl.semaphore_signal(barrier, inc=1, device_id=plane_device(t), device_id_type=MESH)
        for u in range(1, nd):
            pl.semaphore_signal(barrier, inc=1, device_id=depth_device(u), device_id_type=MESH)
        greeted += half - 1 + nd - 1
    for c in load_w2:
        c.start()
    load_pre.start()
    load_inp.start()
    for c in load_w1:
        c.start()

    def halo_copies(send, recv, base):
        return [
            pltpu.make_async_remote_copy(
                src_ref=send.at[i], dst_ref=recv.at[i], send_sem=hs_sem.at[base + i],
                recv_sem=hr_sem.at[base + i], device_id=(other, me_d), device_id_type=MESH,
            )
            for i, other in enumerate((left, right))
        ]

    def pack(dst, src, start, width):
        for p in range(rows):
            dst[p * width : (p + 1) * width, :] = src[p, start : start + width, :]

    def side_inner(src, side, d):
        side[:, 0 : cols - d, 0:ch] = src[:, d:cols, :]
        side[:, d:cols, ch : 2 * ch] = src[:, 0 : cols - d, :]

    def side_fill(side, piece, lo_at, hi_at, width):
        side[:, lo_at : lo_at + width, 0:ch] = piece[0].reshape(rows, width, ch)
        side[:, hi_at : hi_at + width, ch : 2 * ch] = piece[1].reshape(rows, width, ch)

    def input_terms(src, at, lanes, w_v, wl, d, fresh):
        for r in (1, 0, 2):
            lo, hi, first = row_span(rows, d, r)
            term = dot_nt(
                flat(src[first : first + hi - lo, :, at : at + lanes]),
                w_v[r, :, wl : wl + lanes],
            )
            if fresh and r == 1:
                acc[...] = term
            else:
                acc[lo * cols : hi * cols, :] += term

    def scaled(value):
        return value if scatter else value * norm

    def weight_terms(x, src, at, lanes, dw, taps, d):
        for r in range(3):
            lo, hi, first = row_span(rows, d, r)
            term = dot_tn(flat(x[lo:hi]), flat(src[first : first + hi - lo, :, at : at + lanes]))
            for i, c in enumerate(taps):
                k = 3 * r + c
                dw[k * ch : (k + 1) * ch, :] = scaled(term[:, i * ch : (i + 1) * ch])

    def edge_terms(out, lo, hi, taps, width, parts, w_v):
        total = None
        for strip, slot in parts:
            for r, first in taps:
                term = dot_nt(
                    strip[first * width : (first + hi - lo) * width, :],
                    w_v[r, :, slot * ch : (slot + 1) * ch],
                )
                total = term if total is None else total + term
        return total

    if scatter:
        depth = dw1.shape[0] // (nl * nd)
        cut = depth * 2 // 24 * 8
        plane_order = (*range(1, half), 0)

        def chunk(dw, s, parity, start, stop):
            l, d = 2 * (s // nd) + parity, lax.rem(s, nd)
            at = pl.multiple_of((l * nd + d) * depth, 8)
            return dw[pl.ds(at + start, stop - start), :]

        def remote(src, dst, send, recv, device):
            return pltpu.make_async_remote_copy(
                src_ref=src, dst_ref=dst, send_sem=send, recv_sem=recv,
                device_id=device, device_id_type=MESH,
            )

        def pair_copy(g, t):
            ps, pr = sums[g][:2]
            part = pl.ds(lax.rem(my_chip + t, half) * nd, nd)
            sibling = (me_l + 1 - 2 * core, me_d)
            return remote(ps.at[part], pr.at[part], p_ssem.at[g, t], p_rsem.at[g, t], sibling)

        def plane_copy(g, t):
            s, r = sums[g][2:4]
            part = pl.ds(lax.rem(my_chip + t, half) * nd, nd)
            return remote(
                s.at[part], r.at[pl.ds(t * nd, nd)],
                a_ssem.at[g, t], a_rsem.at[g, t], plane_device(t),
            )

        def plane_depth_copy(g, u):
            s, r = sums[g][4:6]
            return remote(s.at[u], r.at[u], b_ssem.at[g, u], b_rsem.at[g, u], depth_device(u))

        def depth_copy(g, u):
            s, r = sums[g][6:8]
            return remote(s.at[u], r.at[u], c_ssem.at[g, u], c_rsem.at[g, u], depth_device(u))

        def depth_plane_copy(g, t):
            s, r = sums[g][8:10]
            return remote(s.at[t], r.at[t], d_ssem.at[g, t], d_rsem.at[g, t], plane_device(t))

        def pair_send(g, dw):
            ps = sums[g][0]
            for t in plane_order:
                for d in range(nd):
                    s = lax.rem(my_chip + t, half) * nd + d
                    ps[s] = chunk(dw, s, 1 - core, 0, depth).astype(BF16)
                pair_copy(g, t).start()

        def chip_sum(g, dw, s, start, stop):
            pr = sums[g][1]
            return chunk(dw, s, core, start, stop) + pr[s, start:stop, :].astype(F32)

        def first_stage(g, dw):
            plane_s, depth_s = sums[g][2], sums[g][6]
            for t in plane_order:
                pair_copy(g, t).wait()
                if t == 0:
                    continue
                for d in range(nd):
                    s = lax.rem(my_chip + t, half) * nd + d
                    plane_s[s] = chip_sum(g, dw, s, 0, cut).astype(BF16)
                plane_copy(g, t).start()
            for u in range(1, nd):
                for c in range(half):
                    s = c * nd + lax.rem(me_d + u, nd)
                    depth_s[u, c] = chip_sum(g, dw, s, cut, depth).astype(BF16)
                depth_copy(g, u).start()

        def plane_sum(g, dw, d):
            total = chip_sum(g, dw, my_chip * nd + d, 0, cut)
            for t in range(1, half):
                total += sums[g][3][t * nd + d].astype(F32)
            return total

        def depth_sum(g, dw, c):
            total = chip_sum(g, dw, c * nd + me_d, cut, depth)
            for u in range(1, nd):
                total += sums[g][7][u, c].astype(F32)
            return total

        def second_stage(g, dw):
            for t in range(1, half):
                plane_copy(g, t).wait()
            for u in range(1, nd):
                sums[g][4][u] = plane_sum(g, dw, lax.rem(me_d + u, nd)).astype(BF16)
                plane_depth_copy(g, u).start()
            for u in range(1, nd):
                depth_copy(g, u).wait()
            for t in range(1, half):
                c = lax.rem(my_chip + t, half)
                sums[g][8][t] = depth_sum(g, dw, c).astype(BF16)
                depth_plane_copy(g, t).start()

        def last_stage(g, dw, out):
            total = plane_sum(g, dw, me_d)
            for u in range(1, nd):
                plane_depth_copy(g, u).wait()
                total += sums[g][5][u].astype(F32)
            for i in range(2):
                out[pl.ds(i, cut, stride=2), :] = total[:, i * ch // 2 : (i + 1) * ch // 2] * norm
            total = depth_sum(g, dw, my_chip)
            for t in range(1, half):
                depth_plane_copy(g, t).wait()
                total += sums[g][9][t].astype(F32)
            for i in range(2):
                out[pl.ds(2 * cut + i, depth - cut, stride=2), :] = (
                    total[:, i * ch // 2 : (i + 1) * ch // 2] * norm
                )

    load_cot.wait()
    pack(sa.at[0], cot_v, rest, first_d)
    pack(sa.at[1], cot_v, cols - second_d, first_d)
    pack(sb.at[0], cot_v, 0, rest)
    pack(sb.at[1], cot_v, cols - rest, rest)
    pl.semaphore_wait(barrier, greeted)
    halo_a = halo_copies(sa, ra, 0)
    halo_b = halo_copies(sb, rb, 2)
    for c in halo_a + halo_b:
        c.start()

    @section
    def _():
        side_inner(cot_v, side2, second_d)
        pack(cot_e.at[0], cot_v, 0, first_d)
        pack(cot_e.at[1], cot_v, cols - first_d, first_d)
        pack(cot_e.at[2], cot_v, second_d, first_d)
        pack(cot_e.at[3], cot_v, cols - first_d - second_d, first_d)

    for c in load_w2:
        c.wait()
    strips = ((0, 2, 2, 0, 1), (1, 2, 3, 1, 0))

    @section
    def _():
        for e, own, other, slot, _ in strips:
            for lo, hi, taps in row_blocks(rows, second_d):
                acc_e[e, lo * first_d : hi * first_d, :] = edge_terms(
                    None, lo, hi, taps, first_d,
                    ((cot_e.at[e], own), (cot_e.at[other], slot)), w2_v,
                )

    @section
    def _():
        input_terms(side2, 2 * ch, ch, w2_v, 2 * ch, second_d, True)

    load_pre.wait()

    @section
    def _():
        pre_v[...] = jnp.maximum(pre_v[...], jnp.zeros((), BF16))
        pack(pre_e.at[0], pre_v, 0, first_d)
        pack(pre_e.at[1], pre_v, cols - first_d, first_d)
        weight_terms(pre_v, side2, 2 * ch, ch, dw2, (1,), second_d)

    for c in halo_a:
        c.wait()

    @section
    def _():
        for e, _, _, _, slot in strips:
            for lo, hi, taps in row_blocks(rows, second_d):
                part = slice(lo * first_d, hi * first_d)
                grad = acc_e[e, part, :] + edge_terms(
                    None, lo, hi, taps, first_d, ((ra.at[1 - e], slot),), w2_v
                )
                sc[e, part, :] = jnp.where(pre_e[e, part, :] > 0, grad, F32(0.0)).astype(BF16)

    halo_c = halo_copies(sc, rc, 4)
    for c in halo_c:
        c.start()

    @section
    def _():
        side_fill(side2, ra, cols - first_d, 0, first_d)

    for c in halo_b:
        c.wait()

    @section
    def _():
        side_fill(side2, rb, cols - second_d, first_d, rest)

    @section
    def _():
        input_terms(side2, 0, 2 * ch, w2_v, 0, second_d, False)

    @section
    def _():
        grad = jnp.where(flat(pre_v[...]) > 0, acc[...], F32(0.0)).astype(BF16)
        lg_v[...] = grad.reshape(rows, cols, ch)

    @section
    def _():
        weight_terms(pre_v, side2, 0, 2 * ch, dw2, (0, 2), second_d)

    if scatter:
        pair_send(1, dw2)
    load_inp.wait()

    @section
    def _():
        zero = jnp.zeros((rows, first_d, ch), BF16)
        side1[:, cols - first_d : cols, 0:ch] = zero
        side1[:, 0:first_d, ch : 2 * ch] = zero
        side_inner(lg_v, side1, first_d)
        pack(inp_e.at[0], inp_v, 0, first_d)
        pack(inp_e.at[1], inp_v, cols - first_d, first_d)

    @section
    def _():
        weight_terms(inp_v, side1, 0, 3 * ch, dw1, (0, 2, 1), first_d)

    if scatter:
        first_stage(1, dw2)
    for c in halo_c:
        c.wait()

    @section
    def _():
        for r in range(3):
            lo, hi, first = row_span(rows, first_d, r)
            for e, c in ((1, 0), (0, 2)):
                k = 3 * r + c
                term = dot_tn(
                    inp_e[e, lo * first_d : hi * first_d, :],
                    rc[1 - e, first * first_d : (first + hi - lo) * first_d, :],
                )
                dw1[k * ch : (k + 1) * ch, :] += scaled(term)

    if scatter:
        pair_send(0, dw1)

    @section
    def _():
        side_fill(side1, rc, cols - first_d, 0, first_d)

    for c in load_w1:
        c.wait()
    if scatter:
        first_stage(0, dw1)

    @section
    def _():
        input_terms(side1, 0, 3 * ch, w1_v, 0, first_d, True)
        ig_out[0] = acc[...].astype(BF16).reshape(rows, cols, ch)

    if scatter:
        second_stage(1, dw2)
        second_stage(0, dw1)
        last_stage(1, dw2, g2_out)
        last_stage(0, dw1, g1_out)


def emit_kernel(*refs):
    count = len(refs) // 2
    copies = [
        pltpu.make_async_copy(refs[i], refs[count + i], refs[-1].at[i]) for i in range(count)
    ]
    for c in copies:
        c.start()
    for c in copies:
        c.wait()


def emit(*values):
    any_spec = pl.BlockSpec(memory_space=pl.ANY)
    vmem_spec = pl.BlockSpec(memory_space=pltpu.VMEM)
    return pl.pallas_call(
        emit_kernel,
        out_shape=[jax.ShapeDtypeStruct(v.shape, v.dtype) for v in values],
        in_specs=[vmem_spec] * len(values),
        out_specs=[any_spec] * len(values),
        scratch_shapes=[pltpu.SemaphoreType.DMA((len(values),))],
        name="emit",
    )(*(pltpu.with_memory_space_constraint(v, pltpu.VMEM) for v in values))


def local(nl, nd, inputs, pre_act, cotangent, first_weight, second_weight):
    _, rows, cols, ch = inputs.shape
    taps_rows = first_weight.shape[0]
    norm = float(rows * cols * nl * inputs.shape[0] * nd) ** -0.5
    devices = nl * nd
    depth = taps_rows // devices
    scatter = nl % 2 == 0 and taps_rows % devices == 0 and depth % 8 == 0 and depth >= 16
    slots = devices // 2
    vm = pltpu.VMEM
    dma = pltpu.SemaphoreType.DMA
    field = vm((rows, cols, ch), BF16)
    weights = vm((3, ch, 3 * ch), BF16)
    side = vm((rows, cols, 3 * ch), BF16)
    rest = SECOND_SPREAD - FIRST_SPREAD

    def strip(count, width, dtype=BF16):
        return vm((count, rows * width, ch), dtype)

    scratch = [field] * 2 + [weights] * 2 + [side] * 2 + [vm((rows * cols, ch), F32)]
    scratch += [strip(4, FIRST_SPREAD), strip(2, FIRST_SPREAD), strip(2, FIRST_SPREAD)]
    scratch += [strip(2, FIRST_SPREAD, F32)]
    scratch += [dma((3,)), dma((9,)), dma((9,))]
    scratch += [strip(2, FIRST_SPREAD)] * 2 + [strip(2, rest)] * 2 + [strip(2, FIRST_SPREAD)] * 2
    scratch += [dma((6,)), dma((6,))]
    if scatter:
        half = nl // 2
        cut = depth * 2 // 24 * 8
        scratch += [vm((taps_rows, ch), F32)] * 2
        for _ in range(2):
            scratch += [vm((slots, depth, ch), BF16)] * 2
            scratch += [vm((slots, cut, ch), BF16)] * 2
            scratch += [vm((nd, cut, ch), BF16)] * 2
            scratch += [vm((nd, half, depth - cut, ch), BF16)] * 2
            scratch += [vm((half, depth - cut, ch), BF16)] * 2
        for count in (half, half, nd, nd, half):
            scratch += [dma((2, count))] * 2
        grad_shape = (2 * depth, ch // 2)
    else:
        grad_shape = (taps_rows, ch)
    any_spec = pl.BlockSpec(memory_space=pl.ANY)
    vmem_spec = pl.BlockSpec(memory_space=pltpu.VMEM)
    place = vm if scatter else jax.ShapeDtypeStruct
    ig, g1, g2 = pl.pallas_call(
        functools.partial(kernel, nl, nd, scatter, norm),
        out_shape=(
            place(inputs.shape, BF16),
            place(grad_shape, F32),
            place(grad_shape, F32),
        ),
        in_specs=[any_spec] * 5,
        out_specs=(vmem_spec, vmem_spec, vmem_spec),
        scratch_shapes=scratch,
        compiler_params=pltpu.CompilerParams(
            collective_id=0, has_side_effects=True, vmem_limit_bytes=62 * 1024 * 1024
        ),
        name="conv_backward",
    )(inputs, pre_act, cotangent, first_weight, second_weight)
    if scatter:
        ig, g1, g2 = emit(ig, g1, g2)
    g1, g2 = g1.reshape(-1), g2.reshape(-1)
    if not scatter:
        g1, g2 = (lax.psum_scatter(g, "lon", scatter_dimension=0, tiled=True) for g in (g1, g2))
        g1, g2 = (lax.psum_scatter(g, "dp", scatter_dimension=0, tiled=True) for g in (g1, g2))
    return ig, g1, g2


def solution(mesh):
    in_specs = (
        P("dp", None, "lon", None),
        P("dp", None, "lon", None),
        P("dp", None, "lon", None),
        P(),
        P(),
    )
    out_specs = (P("dp", None, "lon", None), P(("lon", "dp")), P(("lon", "dp")))
    step = functools.partial(local, mesh.shape["lon"], mesh.shape["dp"])
    return jax.shard_map(step, mesh=mesh, in_specs=in_specs, out_specs=out_specs, check_vma=False)
```

time: 40.6 us -> 34.3 us (0.84)
  Pallas kernels: 39.8 us -> 33.5 us
    pallas_call x1, Pallas kernels: 38.9 us -> 32.6 us  [local(): pl.pallas_call(functools.partial(kernel, nl, nd, scatter, norm), out_shap...]
where the time goes in v3:
time: 34.3 us; the launch traced here: 34.2 us
  Pallas kernels  33.5 us (98%)
  between operations  0.64 us (2%)
    pallas_call x1, Pallas kernels, local(): pl.pallas_call(functools.partial(kernel, nl, nd, scatter, norm), out_shap...  32.6 us
    pallas_call x1, Pallas kernels, emit(): pl.pallas_call(emit_kernel, out_shape=[jax.ShapeDtypeStruct(v.shape, v.dt...  0.94 us

profile of v3, /device:TPU:0, one launch (start us, length us, event | category | flops | bytes accessed | tf_op | source)
XLA Modules:
  0.0 34.2 jit_solution(2052157889100253257)
XLA Ops:
  0.6 32.6 %conv_backward.1 = (bf16[1,32,48,256]{3,2,1,0:T(8,128)(2,1)S(1)}, f32[144,128]{1,0:T(8,128)S(1)}, f32[144,128]{1,0:T(8,128)S(1)}) custom-call(bf16[1,32,48,256]{3,2,1,0:T(8,128)(2,1)} %refs_0_.1, bf16[1,32,48,256]{3,2,1,0:T(8,128)(2,1)} %refs_1_.1, bf16[1,32,48,256]{3,2,1,0:T(8,128)(2,1)} %refs_2_.1, bf16[2304,256]{1,0:T(8,128)(2,1)} %refs_3_.1, ...), custom_call_target="tpu_custom_call" | custom-call | tf_op jit(solution)/shard_map/conv_backward/pallas_call | solution.py:501
  33.2 0.9 %emit.1 = (bf16[1,32,48,256]{3,2,1,0:T(8,128)(2,1)}, f32[144,128]{1,0:T(8,128)}, f32[144,128]{1,0:T(8,128)}) custom-call(bf16[1,32,48,256]{3,2,1,0:T(8,128)(2,1)S(1)} %get-tuple-element.9.refs_0_, f32[144,128]{1,0:T(8,128)S(1)} %get-tuple-element.10.refs_1_, f32[144,128]{1,0:T(8,128)S(1)} %get-tuple-element.11.refs_2_), custom_call_target="tpu_custom_call" | custom-call | tf_op jit(solution)/shard_map/emit/pallas_call | solution.py:449

commit v4 on v3

v4 whole, which is shorter than its diff:
```python
import functools
import typing

import jax
import jax.numpy as jnp
from jax import lax
from jax.experimental import pallas as pl
from jax.experimental.pallas import tpu as pltpu
from jax.sharding import PartitionSpec as P

FIRST_SPREAD = 12
SECOND_SPREAD = 18
MESH = pl.DeviceIdType.MESH
F32 = jnp.float32
BF16 = jnp.bfloat16
LANE_SLOT = (0, 2, 1)


def row_span(rows, dilation, r):
    if r == 0:
        return 0, rows - dilation, dilation
    if r == 1:
        return 0, rows, 0
    return dilation, rows, 0


class Bank(typing.NamedTuple):
    ep_s: typing.Any
    ep_r: typing.Any
    ez_s: typing.Any
    ez_r: typing.Any
    ex_s: typing.Any
    ex_r: typing.Any
    lp_s: typing.Any
    lp_r: typing.Any
    pa_s: typing.Any
    pa_r: typing.Any
    pb_s: typing.Any
    pb_r: typing.Any
    za_s: typing.Any
    za_r: typing.Any
    zb_s: typing.Any
    zb_r: typing.Any
    ep_sem: typing.Any
    ez_sem: typing.Any
    ex_sem: typing.Any
    lps_sem: typing.Any
    lpr_sem: typing.Any
    pas_sem: typing.Any
    par_sem: typing.Any
    pbs_sem: typing.Any
    pbr_sem: typing.Any
    za_sem: typing.Any
    zb_sem: typing.Any


def first_rows(depth):
    return depth * 8 // 72 * 8, depth * 7 // 72 * 8


def bank_scratch(nl, nd, depth, ch, cut):
    half = nl // 2
    dma = pltpu.SemaphoreType.DMA

    def buf(*shape):
        return pltpu.VMEM((*shape, ch), BF16)

    return [
        *[buf(nd, depth)] * 4, buf(depth), buf(half, depth),
        *[buf(half - 1, nd, depth)] * 2,
        buf(nd, half - 1, cut), buf(nd, half, cut), *[buf(nd, cut)] * 2,
        *[buf(nd, half - 1, depth - cut)] * 2, buf(half - 1, depth - cut), buf(half, depth - cut),
        dma((2,)), dma((2,)), dma((2,)), dma, dma((half - 1,)),
        dma((nd,)), dma((nd,)), dma((nd,)), dma, dma((2,)), dma((2,)),
    ]


def early_owners(nl, nd, depth, ch):
    table = []
    for parity in range(2):
        row = []
        for d in range(nd):
            chips = []
            for chip in range(nl // 2):
                start = ((2 * chip + parity) * nd + d) * depth
                taps = {start // ch % 3, (start + depth - 1) // ch % 3}
                if taps == {1} and depth <= ch:
                    chips.append(chip)
            if len(chips) != 1:
                return None
            row.append(chips[0])
        table.append(row)
    return table


def row_blocks(rows, dilation):
    cuts = sorted({0, dilation, rows - dilation, rows})
    blocks = []
    for lo, hi in zip(cuts, cuts[1:]):
        taps = []
        for r in range(3):
            start, stop, first = row_span(rows, dilation, r)
            if start <= lo and hi <= stop:
                taps.append((r, first + lo - start))
        blocks.append((lo, hi, taps))
    return blocks


def dot_nt(a, b):
    return lax.dot_general(a, b, (((1,), (1,)), ((), ())), preferred_element_type=F32)


def dot_tn(a, b):
    return lax.dot_general(a, b, (((0,), (0,)), ((), ())), preferred_element_type=F32)


def flat(v):
    return v.reshape(-1, v.shape[-1])


def kernel(nl, nd, owners, norm, *refs):
    refs = list(refs)
    scatter = owners is not None

    def take(count):
        taken = refs[:count]
        del refs[:count]
        return taken

    inp, pre, cot, w1, w2 = take(5)
    ig_out, g1_out, g2_out = take(3)
    pre_v, inp_v, w1_v, w2_v, side2, side1, acc = take(7)
    cot_e, pre_e, inp_e, acc_e, cot_f, pre_f, acc_f, lg_f = take(8)
    in_sem, w1_sem, w2_sem = take(3)
    sa, ra, sb, rb, sc, rc, hs_sem, hr_sem = take(8)
    if scatter:
        dw1, dw2 = take(2)
        banks = [Bank(*take(len(Bank._fields))) for _ in range(2)]
        (greet,) = take(1)
    else:
        dw1, dw2 = g1_out, g2_out

    rows, cols, ch = pre_v.shape
    first_d, second_d = FIRST_SPREAD, SECOND_SPREAD
    rest = second_d - first_d
    me_l, me_d = lax.axis_index("lon"), lax.axis_index("dp")
    left, right = lax.rem(me_l + nl - 1, nl), lax.rem(me_l + 1, nl)
    half = nl // 2
    core = lax.rem(me_l, 2)
    my_chip = me_l // 2
    cot_v = side2.at[:, :, pl.ds(2 * ch, ch)]
    lg_v = side1.at[:, :, pl.ds(2 * ch, ch)]
    section = pl.when(me_l >= 0)

    def plane_device(t):
        return (2 * lax.rem(my_chip + t, half) + core, me_d)

    def depth_device(u):
        return (me_l, lax.rem(me_d + u, nd))

    load_cot = pltpu.make_async_copy(cot.at[0], cot_v, in_sem.at[0])
    load_pre = pltpu.make_async_copy(pre.at[0], pre_v, in_sem.at[1])
    load_inp = pltpu.make_async_copy(inp.at[0], inp_v, in_sem.at[2])

    def weight_loads(w, w_v, sem):
        return [
            pltpu.make_async_copy(
                w.at[pl.ds(k * ch, ch)],
                w_v.at[k // 3, :, pl.ds(LANE_SLOT.index(k % 3) * ch, ch)],
                sem,
            )
            for k in range(9)
        ]

    load_w2 = weight_loads(w2, w2_v, w2_sem)
    load_w1 = weight_loads(w1, w1_v, w1_sem)

    def landed(ref, sem):
        pltpu.make_async_copy(ref, ref, sem).wait()

    load_cot.start()

    barrier = pltpu.get_barrier_semaphore()
    for other in (left, right):
        pl.semaphore_signal(barrier, inc=1, device_id=(other, me_d), device_id_type=MESH)
    greeted = 2
    if scatter:
        for t in range(1, half):
            pl.semaphore_signal(barrier, inc=1, device_id=plane_device(t), device_id_type=MESH)
        for d in range(1, nd):
            @pl.when(me_d < d)
            def _(d=d):
                pl.semaphore_signal(barrier, inc=1, device_id=(me_l, d), device_id_type=MESH)
        greeted += half - 1 + me_d
    for c in load_w2:
        c.start()
    load_pre.start()
    load_inp.start()
    for c in load_w1:
        c.start()

    def halo_copies(send, recv, base):
        return [
            pltpu.make_async_remote_copy(
                src_ref=send.at[i], dst_ref=recv.at[i], send_sem=hs_sem.at[base],
                recv_sem=hr_sem.at[base], device_id=(other, me_d), device_id_type=MESH,
            )
            for i, other in enumerate((left, right))
        ]

    def pack(dst, src, start, width):
        for p in range(rows):
            dst[p * width : (p + 1) * width, :] = src[p, start : start + width, :]

    def side_inner(src, side, d):
        zero = jnp.zeros((rows, d, ch), BF16)
        side[:, cols - d : cols, 0:ch] = zero
        side[:, 0:d, ch : 2 * ch] = zero
        side[:, 0 : cols - d, 0:ch] = src[:, d:cols, :]
        side[:, d:cols, ch : 2 * ch] = src[:, 0 : cols - d, :]

    def side_fill(side, piece, lo_at, hi_at, width):
        side[:, lo_at : lo_at + width, 0:ch] = piece[0].reshape(rows, width, ch)
        side[:, hi_at : hi_at + width, ch : 2 * ch] = piece[1].reshape(rows, width, ch)

    def input_terms(src, at, lanes, w_v, wl, d, fresh):
        for r in (1, 0, 2):
            lo, hi, first = row_span(rows, d, r)
            term = dot_nt(
                flat(src[first : first + hi - lo, :, at : at + lanes]),
                w_v[r, :, wl : wl + lanes],
            )
            if fresh and r == 1:
                acc[...] = term
            else:
                acc[lo * cols : hi * cols, :] += term

    def scaled(value):
        return value if scatter else value * norm

    def weight_terms(x, src, at, lanes, dw, taps, d):
        for r in range(3):
            lo, hi, first = row_span(rows, d, r)
            term = dot_tn(flat(x[lo:hi]), flat(src[first : first + hi - lo, :, at : at + lanes]))
            for i, c in enumerate(taps):
                k = 3 * r + c
                dw[k * ch : (k + 1) * ch, :] = scaled(term[:, i * ch : (i + 1) * ch])

    def edge_terms(lo, hi, taps, width, parts, w_v):
        total = None
        for strip, slot in parts:
            for r, first in taps:
                term = dot_nt(
                    strip[first * width : (first + hi - lo) * width, :],
                    w_v[r, :, slot * ch : (slot + 1) * ch],
                )
                total = term if total is None else total + term
        return total

    if scatter:
        depth = dw1.shape[0] // (nl * nd)

        def owner(parity, d):
            total = 0
            for dd in range(nd):
                low, high = owners[0][dd], owners[1][dd]
                total = jnp.where(d == dd, low + parity * (high - low), total)
            return total

        def late(parity, d, i):
            return i + jnp.where(owner(parity, d) <= i, 1, 0)

        def chunk(dw, chip, d, parity, start, stop):
            at = pl.multiple_of(((2 * chip + parity) * nd + d) * depth, 8)
            return dw[pl.ds(at + start, stop - start), :]

        def remote(src, dst, send, recv, device):
            return pltpu.make_async_remote_copy(
                src_ref=src, dst_ref=dst, send_sem=send, recv_sem=recv,
                device_id=device, device_id_type=MESH,
            )

        def seen_from(chip):
            return lax.rem(my_chip - chip + half, half)

        sibling = (me_l + 1 - 2 * core, me_d)
        mine = owner(core, me_d)

        def early_pair(g, dw):
            b = banks[g]
            for d in range(nd):
                chip = owner(1 - core, d)
                b.ep_s[d] = chunk(dw, chip, d, 1 - core, 0, depth).astype(BF16)
            remote(b.ep_s, b.ep_r, b.ep_sem.at[0], b.ep_sem.at[1], sibling).start()

        def early_chip_sum(b, dw, d):
            return chunk(dw, owner(core, d), d, core, 0, depth) + b.ep_r[d].astype(F32)

        def early_depth(g, dw):
            b = banks[g]
            landed(b.ep_r, b.ep_sem.at[1])
            for u in range(1, nd):
                b.ez_s[u] = early_chip_sum(b, dw, lax.rem(me_d + u, nd)).astype(BF16)
                remote(
                    b.ez_s.at[u], b.ez_r.at[u], b.ez_sem.at[0], b.ez_sem.at[1], depth_device(u)
                ).start()

        def early_sum(b, dw):
            total = early_chip_sum(b, dw, me_d)
            for u in range(1, nd):
                total += b.ez_r[u].astype(F32)
            return total

        def early_plane(g, dw):
            b = banks[g]
            landed(b.ez_r.at[pl.ds(1, nd - 1)], b.ez_sem.at[1])

            @pl.when(my_chip != mine)
            def _():
                b.ex_s[...] = early_sum(b, dw).astype(BF16)
                remote(
                    b.ex_s, b.ex_r.at[seen_from(mine)], b.ex_sem.at[0], b.ex_sem.at[1],
                    (2 * mine + core, me_d),
                ).start()

        def late_pair(g, dw):
            b = banks[g]
            for i in range(half - 1):
                for d in range(nd):
                    chip = late(1 - core, d, i)
                    b.lp_s[i, d] = chunk(dw, chip, d, 1 - core, 0, depth).astype(BF16)
                remote(b.lp_s.at[i], b.lp_r.at[i], b.lps_sem, b.lpr_sem.at[i], sibling).start()

        def late_chip_sum(b, dw, chip, i, d, start, stop):
            return chunk(dw, chip, d, core, start, stop) + b.lp_r[i, d, start:stop, :].astype(F32)

        def late_first(g, dw):
            b = banks[g]
            for i in range(half - 1):
                landed(b.lp_r.at[i], b.lpr_sem.at[i])
                for d in range(nd):
                    chip = late(core, d, i)

                    @pl.when(chip != my_chip)
                    def _(i=i, d=d, chip=chip):
                        b.pa_s[d, i] = late_chip_sum(b, dw, chip, i, d, 0, b.pa_s.shape[2]).astype(BF16)
                        remote(
                            b.pa_s.at[d, i], b.pa_r.at[d, seen_from(chip)],
                            b.pas_sem.at[d], b.par_sem.at[d], (2 * chip + core, me_d),
                        ).start()
            for u in range(1, nd):
                d = lax.rem(me_d + u, nd)
                for i in range(half - 1):
                    chip = late(core, d, i)
                    b.za_s[u, i] = late_chip_sum(b, dw, chip, i, d, b.pa_s.shape[2], depth).astype(BF16)
                remote(
                    b.za_s.at[u], b.za_r.at[u], b.za_sem.at[0], b.za_sem.at[1], depth_device(u)
                ).start()

        def plane_sum(b, dw, d):
            i = my_chip - jnp.where(owner(core, d) < my_chip, 1, 0)
            total = late_chip_sum(b, dw, my_chip, i, d, 0, b.pa_s.shape[2])
            for t in range(1, half):
                total += b.pa_r[d, t].astype(F32)
            return total

        def depth_sum(b, dw, chip, i):
            total = late_chip_sum(b, dw, chip, i, me_d, b.pa_s.shape[2], depth)
            for u in range(1, nd):
                total += b.za_r[u, i].astype(F32)
            return total

        def late_second_plane(g, dw):
            b = banks[g]
            for u in (*range(1, nd), 0):
                d = lax.rem(me_d + u, nd)

                @pl.when(owner(core, d) != my_chip)
                def _(u=u, d=d):
                    landed(b.pa_r.at[d, pl.ds(1, half - 1)], b.par_sem.at[d])
                    if u:
                        b.pb_s[u] = plane_sum(b, dw, d).astype(BF16)
                        remote(
                            b.pb_s.at[u], b.pb_r.at[u], b.pbs_sem.at[u], b.pbr_sem,
                            depth_device(u),
                        ).start()

        def late_second_depth(g, dw):
            b = banks[g]
            landed(b.za_r.at[pl.ds(1, nd - 1)], b.za_sem.at[1])
            for i in range(half - 1):
                chip = late(core, me_d, i)

                @pl.when(chip != my_chip)
                def _(i=i, chip=chip):
                    b.zb_s[i] = depth_sum(b, dw, chip, i).astype(BF16)
                    remote(
                        b.zb_s.at[i], b.zb_r.at[seen_from(chip)],
                        b.zb_sem.at[0], b.zb_sem.at[1], (2 * chip + core, me_d),
                    ).start()

        def put(out, total, start, count):
            for i in range(2):
                out[pl.ds(2 * start + i, count, stride=2), :] = (
                    total[:, i * ch // 2 : (i + 1) * ch // 2] * norm
                )

        def last_stage(g, dw, out):
            b = banks[g]

            @pl.when(my_chip == mine)
            def _():
                total = early_sum(b, dw)
                landed(b.ex_r.at[pl.ds(1, half - 1)], b.ex_sem.at[1])
                for t in range(1, half):
                    total += b.ex_r[t].astype(F32)
                put(out, total, 0, depth)
                landed(b.zb_s, b.zb_sem.at[0])

            @pl.when(my_chip != mine)
            def _():
                landed(b.pb_r.at[pl.ds(1, nd - 1)], b.pbr_sem)
                total = plane_sum(b, dw, me_d)
                for u in range(1, nd):
                    total += b.pb_r[u].astype(F32)
                put(out, total, 0, b.pa_s.shape[2])
                landed(b.zb_r.at[pl.ds(1, half - 1)], b.zb_sem.at[1])
                total = depth_sum(b, dw, my_chip, my_chip - jnp.where(mine < my_chip, 1, 0))
                for t in range(1, half):
                    total += b.zb_r[t].astype(F32)
                put(out, total, b.pa_s.shape[2], depth - b.pa_s.shape[2])
                landed(b.zb_s.at[pl.ds(0, half - 2)], b.zb_sem.at[0])
                landed(b.ex_s, b.ex_sem.at[0])

            landed(b.ep_s, b.ep_sem.at[0])
            landed(b.ez_s.at[pl.ds(1, nd - 1)], b.ez_sem.at[0])
            landed(b.lp_s, b.lps_sem)
            landed(b.za_s.at[pl.ds(1, nd - 1)], b.za_sem.at[0])
            for u in range(nd):
                d = lax.rem(me_d + u, nd)

                @pl.when(owner(core, d) == my_chip)
                def _(d=d):
                    landed(b.pa_s.at[d], b.pas_sem.at[d])

                @pl.when(owner(core, d) != my_chip)
                def _(u=u, d=d):
                    landed(b.pa_s.at[d, pl.ds(0, half - 2)], b.pas_sem.at[d])
                    if u:
                        landed(b.pb_s.at[u], b.pbs_sem.at[u])

    load_cot.wait()
    pack(sa.at[0], cot_v, rest, first_d)
    pack(sa.at[1], cot_v, cols - second_d, first_d)
    pack(sb.at[0], cot_v, 0, rest)
    pack(sb.at[1], cot_v, cols - rest, rest)
    pl.semaphore_wait(barrier, greeted)
    if scatter:
        for d in range(nd - 1):
            @pl.when(me_d > d)
            def _(d=d):
                pl.semaphore_signal(greet, inc=1, device_id=(me_l, d), device_id_type=MESH)
    halo_a = halo_copies(sa, ra, 0)
    halo_b = halo_copies(sb, rb, 1)
    for c in halo_a + halo_b:
        c.start()

    outer = (cot_e, acc_e, first_d, (0, cols - first_d), (second_d, cols - first_d - second_d))
    inner = (
        cot_f, acc_f, rest, (first_d, cols - second_d),
        (first_d + second_d, cols - 2 * second_d),
    )

    def strip_packs(group):
        strips, _, width, own, other = group
        for e in range(2):
            pack(strips.at[e], cot_v, own[e], width)
            pack(strips.at[2 + e], cot_v, other[e], width)

    def strip_start(group):
        strips, sums_e, width, _, _ = group
        for e in range(2):
            for lo, hi, taps in row_blocks(rows, second_d):
                sums_e[e, lo * width : hi * width, :] = edge_terms(
                    lo, hi, taps, width, ((strips.at[e], 2), (strips.at[2 + e], e)), w2_v
                )

    def strip_finish(group, halo, pre_s, out):
        _, sums_e, width, _, _ = group
        for e in range(2):
            for lo, hi, taps in row_blocks(rows, second_d):
                part = slice(lo * width, hi * width)
                grad = sums_e[e, part, :] + edge_terms(
                    lo, hi, taps, width, ((halo.at[1 - e], 1 - e),), w2_v
                )
                out[e, part, :] = jnp.where(pre_s[e, part, :] > 0, grad, F32(0.0)).astype(BF16)

    def strip_place(group, value):
        _, _, width, own, _ = group
        for e in range(2):
            side1[:, own[e] : own[e] + width, 2 * ch : 3 * ch] = value[e].reshape(rows, width, ch)

    def edge_update(dw, d, groups):
        for r in range(3):
            lo, hi, first = row_span(rows, d, r)
            for e, c in ((1, 0), (0, 2)):
                total = None
                for own, halo, width in groups:
                    term = dot_tn(
                        own[e, lo * width : hi * width, :],
                        halo[1 - e, first * width : (first + hi - lo) * width, :],
                    )
                    total = term if total is None else total + term
                k = 3 * r + c
                dw[k * ch : (k + 1) * ch, :] += scaled(total)

    @section
    def _():
        side_inner(cot_v, side2, second_d)
        strip_packs(outer)
        strip_packs(inner)

    landed(w2_v, w2_sem)

    @section
    def _():
        strip_start(outer)

    load_pre.wait()

    @section
    def _():
        pre_v[...] = jnp.maximum(pre_v[...], jnp.zeros((), BF16))
        for e in range(2):
            pack(pre_e.at[e], pre_v, outer[3][e], first_d)
            pack(pre_f.at[e], pre_v, inner[3][e], rest)

    @section
    def _():
        input_terms(side2, 0, 3 * ch, w2_v, 0, second_d, True)

    @section
    def _():
        grad = jnp.where(flat(pre_v[...]) > 0, acc[...], F32(0.0)).astype(BF16)
        lg_v[...] = grad.reshape(rows, cols, ch)

    @section
    def _():
        weight_terms(pre_v, side2, 0, 3 * ch, dw2, (0, 2, 1), second_d)

    if scatter:
        early_pair(1, dw2)

    @section
    def _():
        strip_start(inner)

    landed(ra, hr_sem.at[0])

    @section
    def _():
        strip_finish(outer, ra, pre_e, sc)

    halo_c = halo_copies(sc, rc, 2)
    for c in halo_c:
        c.start()

    @section
    def _():
        strip_place(outer, sc)

    if scatter:
        @pl.when(me_d < nd - 1)
        def _():
            pl.semaphore_wait(greet, nd - 1 - me_d)

        early_depth(1, dw2)
    landed(rb, hr_sem.at[1])

    @section
    def _():
        strip_finish(inner, rb, pre_f, lg_f)
        strip_place(inner, lg_f)

    @section
    def _():
        edge_update(dw2, second_d, ((pre_e, ra, first_d), (pre_f, rb, rest)))

    if scatter:
        late_pair(1, dw2)
    load_inp.wait()

    @section
    def _():
        side_inner(lg_v, side1, first_d)
        pack(inp_e.at[0], inp_v, 0, first_d)
        pack(inp_e.at[1], inp_v, cols - first_d, first_d)

    @section
    def _():
        weight_terms(inp_v, side1, 0, 3 * ch, dw1, (0, 2, 1), first_d)

    if scatter:
        early_pair(0, dw1)
    if scatter:
        late_first(1, dw2)
    if scatter:
        early_depth(0, dw1)
    landed(rc, hr_sem.at[2])

    @section
    def _():
        edge_update(dw1, first_d, ((inp_e, rc, first_d),))

    if scatter:
        late_pair(0, dw1)

    @section
    def _():
        side_fill(side1, rc, cols - first_d, 0, first_d)

    landed(w1_v, w1_sem)
    if scatter:
        late_first(0, dw1)
    if scatter:
        early_plane(1, dw2)

    @section
    def _():
        input_terms(side1, 0, 3 * ch, w1_v, 0, first_d, True)
        ig_out[0] = acc[...].astype(BF16).reshape(rows, cols, ch)

    if scatter:
        late_second_plane(1, dw2)
    if scatter:
        late_second_depth(1, dw2)
    if scatter:
        late_second_plane(0, dw1)
    if scatter:
        late_second_depth(0, dw1)
    if scatter:
        early_plane(0, dw1)
    if scatter:
        last_stage(1, dw2, g2_out)
    if scatter:
        last_stage(0, dw1, g1_out)
    for i, ref in enumerate((sa, sb, sc)):
        landed(ref, hs_sem.at[i])


def emit_kernel(*refs):
    count = len(refs) // 2
    copies = [
        pltpu.make_async_copy(refs[i], refs[count + i], refs[-1].at[i]) for i in range(count)
    ]
    for c in copies:
        c.start()
    for c in copies:
        c.wait()


def emit(*values):
    any_spec = pl.BlockSpec(memory_space=pl.ANY)
    vmem_spec = pl.BlockSpec(memory_space=pltpu.VMEM)
    return pl.pallas_call(
        emit_kernel,
        out_shape=[jax.ShapeDtypeStruct(v.shape, v.dtype) for v in values],
        in_specs=[vmem_spec] * len(values),
        out_specs=[any_spec] * len(values),
        scratch_shapes=[pltpu.SemaphoreType.DMA((len(values),))],
        name="emit",
    )(*(pltpu.with_memory_space_constraint(v, pltpu.VMEM) for v in values))


def local(nl, nd, inputs, pre_act, cotangent, first_weight, second_weight):
    _, rows, cols, ch = inputs.shape
    taps_rows = first_weight.shape[0]
    norm = float(rows * cols * nl * inputs.shape[0] * nd) ** -0.5
    devices = nl * nd
    depth = taps_rows // devices
    even = nl % 2 == 0 and nl >= 6 and nd >= 2
    even = even and taps_rows % devices == 0 and depth % 8 == 0 and depth >= 16
    owners = early_owners(nl, nd, depth, ch) if even else None
    scatter = owners is not None
    vm = pltpu.VMEM
    dma = pltpu.SemaphoreType.DMA
    field = vm((rows, cols, ch), BF16)
    weights = vm((3, ch, 3 * ch), BF16)
    side = vm((rows, cols, 3 * ch), BF16)
    rest = SECOND_SPREAD - FIRST_SPREAD

    def strip(count, width, dtype=BF16):
        return vm((count, rows * width, ch), dtype)

    scratch = [field] * 2 + [weights] * 2 + [side] * 2 + [vm((rows * cols, ch), F32)]
    scratch += [strip(4, FIRST_SPREAD), strip(2, FIRST_SPREAD), strip(2, FIRST_SPREAD)]
    scratch += [strip(2, FIRST_SPREAD, F32)]
    scratch += [strip(4, rest), strip(2, rest), strip(2, rest, F32), strip(2, rest)]
    scratch += [dma((3,)), dma, dma]
    scratch += [strip(2, FIRST_SPREAD)] * 2 + [strip(2, rest)] * 2 + [strip(2, FIRST_SPREAD)] * 2
    scratch += [dma((3,)), dma((3,))]
    if scatter:
        scratch += [vm((taps_rows, ch), F32)] * 2
        for cut in first_rows(depth):
            scratch += bank_scratch(nl, nd, depth, ch, cut)
        scratch += [pltpu.SemaphoreType.REGULAR]
        grad_shape = (2 * depth, ch // 2)
    else:
        grad_shape = (taps_rows, ch)
    any_spec = pl.BlockSpec(memory_space=pl.ANY)
    vmem_spec = pl.BlockSpec(memory_space=pltpu.VMEM)
    place = vm if scatter else jax.ShapeDtypeStruct
    ig, g1, g2 = pl.pallas_call(
        functools.partial(kernel, nl, nd, owners, norm),
        out_shape=(
            place(inputs.shape, BF16),
            place(grad_shape, F32),
            place(grad_shape, F32),
        ),
        in_specs=[any_spec] * 5,
        out_specs=(vmem_spec, vmem_spec, vmem_spec),
        scratch_shapes=scratch,
        compiler_params=pltpu.CompilerParams(
            collective_id=0, has_side_effects=True, vmem_limit_bytes=62 * 1024 * 1024
        ),
        name="conv_backward",
    )(inputs, pre_act, cotangent, first_weight, second_weight)
    if scatter:
        ig, g1, g2 = emit(ig, g1, g2)
    g1, g2 = g1.reshape(-1), g2.reshape(-1)
    if not scatter:
        g1, g2 = (lax.psum_scatter(g, "lon", scatter_dimension=0, tiled=True) for g in (g1, g2))
        g1, g2 = (lax.psum_scatter(g, "dp", scatter_dimension=0, tiled=True) for g in (g1, g2))
    return ig, g1, g2


def solution(mesh):
    in_specs = (
        P("dp", None, "lon", None),
        P("dp", None, "lon", None),
        P("dp", None, "lon", None),
        P(),
        P(),
    )
    out_specs = (P("dp", None, "lon", None), P(("lon", "dp")), P(("lon", "dp")))
    step = functools.partial(local, mesh.shape["lon"], mesh.shape["dp"])
    return jax.shard_map(step, mesh=mesh, in_specs=in_specs, out_specs=out_specs, check_vma=False)
```

time: 34.3 us -> 31.6 us (0.921); the launches traced: 34.2 us -> 31.1 us
  Pallas kernels: 33.5 us -> 30.4 us
    pallas_call x1, Pallas kernels: 32.6 us -> 29.5 us  [local(): pl.pallas_call(functools.partial(kernel, nl, nd, owners, norm), out_shape...]
where the time goes in v4:
time: 31.6 us; the launch traced here: 31.1 us
  Pallas kernels  30.4 us (96%)
  between operations  0.64 us (2%)
    pallas_call x1, Pallas kernels, local(): pl.pallas_call(functools.partial(kernel, nl, nd, owners, norm), out_shape...  29.5 us
    pallas_call x1, Pallas kernels, emit(): pl.pallas_call(emit_kernel, out_shape=[jax.ShapeDtypeStruct(v.shape, v.dt...  0.94 us

profile of v4, /device:TPU:0, one launch (start us, length us, event | category | flops | bytes accessed | tf_op | source)
XLA Modules:
  0.0 31.1 jit_solution(5747476805153589179)
XLA Ops:
  0.6 29.5 %conv_backward.1 = (bf16[1,32,48,256]{3,2,1,0:T(8,128)(2,1)S(1)}, f32[144,128]{1,0:T(8,128)S(1)}, f32[144,128]{1,0:T(8,128)S(1)}) custom-call(bf16[1,32,48,256]{3,2,1,0:T(8,128)(2,1)} %refs_0_.1, bf16[1,32,48,256]{3,2,1,0:T(8,128)(2,1)} %refs_1_.1, bf16[1,32,48,256]{3,2,1,0:T(8,128)(2,1)} %refs_2_.1, bf16[2304,256]{1,0:T(8,128)(2,1)} %refs_3_.1, ...), custom_call_target="tpu_custom_call" | custom-call | tf_op jit(solution)/shard_map/conv_backward/pallas_call | solution.py:713
  30.1 0.9 %emit.1 = (bf16[1,32,48,256]{3,2,1,0:T(8,128)(2,1)}, f32[144,128]{1,0:T(8,128)}, f32[144,128]{1,0:T(8,128)}) custom-call(bf16[1,32,48,256]{3,2,1,0:T(8,128)(2,1)S(1)} %get-tuple-element.9.refs_0_, f32[144,128]{1,0:T(8,128)S(1)} %get-tuple-element.10.refs_1_, f32[144,128]{1,0:T(8,128)S(1)} %get-tuple-element.11.refs_2_), custom_call_target="tpu_custom_call" | custom-call | tf_op jit(solution)/shard_map/emit/pallas_call | solution.py:665

commit v5 on v4

--- a/solution.py
+++ b/solution.py
@@ -592,18 +592,23 @@
 
     @section
     def _():
+        weight_terms(inp_v, side1, 2 * ch, ch, dw1, (1,), first_d)
+
+    if scatter:
+        early_pair(0, dw1)
+    if scatter:
+        late_first(1, dw2)
+
+    @section
+    def _():
         side_inner(lg_v, side1, first_d)
         pack(inp_e.at[0], inp_v, 0, first_d)
         pack(inp_e.at[1], inp_v, cols - first_d, first_d)
 
     @section
     def _():
-        weight_terms(inp_v, side1, 0, 3 * ch, dw1, (0, 2, 1), first_d)
-
-    if scatter:
-        early_pair(0, dw1)
-    if scatter:
-        late_first(1, dw2)
+        weight_terms(inp_v, side1, 0, 2 * ch, dw1, (0, 2), first_d)
+
     if scatter:
         early_depth(0, dw1)
     landed(rc, hr_sem.at[2])

time: 31.6 us -> 30.8 us (0.975); the launches traced: 31.1 us -> 30.6 us
  Pallas kernels: 30.4 us -> 30 us
    pallas_call x1, Pallas kernels: 29.5 us -> 29 us  [local(): pl.pallas_call(functools.partial(kernel, nl, nd, owners, norm), out_shape...]
where the time goes in v5:
time: 30.8 us; the launch traced here: 30.6 us
  Pallas kernels  30 us (97%)
  between operations  0.64 us (2%)
    pallas_call x1, Pallas kernels, local(): pl.pallas_call(functools.partial(kernel, nl, nd, owners, norm), out_shape...  29 us
    pallas_call x1, Pallas kernels, emit(): pl.pallas_call(emit_kernel, out_shape=[jax.ShapeDtypeStruct(v.shape, v.dt...  0.94 us

profile of v5, /device:TPU:0, one launch (start us, length us, event | category | flops | bytes accessed | tf_op | source)
XLA Modules:
  0.0 30.6 jit_solution(14178194713518882427)
XLA Ops:
  0.6 29.0 %conv_backward.1 = (bf16[1,32,48,256]{3,2,1,0:T(8,128)(2,1)S(1)}, f32[144,128]{1,0:T(8,128)S(1)}, f32[144,128]{1,0:T(8,128)S(1)}) custom-call(bf16[1,32,48,256]{3,2,1,0:T(8,128)(2,1)} %refs_0_.1, bf16[1,32,48,256]{3,2,1,0:T(8,128)(2,1)} %refs_1_.1, bf16[1,32,48,256]{3,2,1,0:T(8,128)(2,1)} %refs_2_.1, bf16[2304,256]{1,0:T(8,128)(2,1)} %refs_3_.1, ...), custom_call_target="tpu_custom_call" | custom-call | tf_op jit(solution)/shard_map/conv_backward/pallas_call | solution.py:718
  29.7 0.9 %emit.1 = (bf16[1,32,48,256]{3,2,1,0:T(8,128)(2,1)}, f32[144,128]{1,0:T(8,128)}, f32[144,128]{1,0:T(8,128)}) custom-call(bf16[1,32,48,256]{3,2,1,0:T(8,128)(2,1)S(1)} %get-tuple-element.9.refs_0_, f32[144,128]{1,0:T(8,128)S(1)} %get-tuple-element.10.refs_1_, f32[144,128]{1,0:T(8,128)S(1)} %get-tuple-element.11.refs_2_), custom_call_target="tpu_custom_call" | custom-call | tf_op jit(solution)/shard_map/emit/pallas_call | solution.py:670

commit v6 on v5

--- a/solution.py
+++ b/solution.py
@@ -10,6 +10,7 @@
 
 FIRST_SPREAD = 12
 SECOND_SPREAD = 18
+EMIT_PARTS = 4
 MESH = pl.DeviceIdType.MESH
 F32 = jnp.float32
 BF16 = jnp.bfloat16
@@ -452,8 +453,6 @@
     load_cot.wait()
     pack(sa.at[0], cot_v, rest, first_d)
     pack(sa.at[1], cot_v, cols - second_d, first_d)
-    pack(sb.at[0], cot_v, 0, rest)
-    pack(sb.at[1], cot_v, cols - rest, rest)
     pl.semaphore_wait(barrier, greeted)
     if scatter:
         for d in range(nd - 1):
@@ -462,7 +461,11 @@
                 pl.semaphore_signal(greet, inc=1, device_id=(me_l, d), device_id_type=MESH)
     halo_a = halo_copies(sa, ra, 0)
     halo_b = halo_copies(sb, rb, 1)
-    for c in halo_a + halo_b:
+    for c in halo_a:
+        c.start()
+    pack(sb.at[0], cot_v, 0, rest)
+    pack(sb.at[1], cot_v, cols - rest, rest)
+    for c in halo_b:
         c.start()
 
     outer = (cot_e, acc_e, first_d, (0, cols - first_d), (second_d, cols - first_d - second_d))
@@ -655,13 +658,18 @@
 
 def emit_kernel(*refs):
     count = len(refs) // 2
-    copies = [
-        pltpu.make_async_copy(refs[i], refs[count + i], refs[-1].at[i]) for i in range(count)
-    ]
-    for c in copies:
-        c.start()
-    for c in copies:
-        c.wait()
+    sem = refs[-1]
+    for i in range(count):
+        src, dst = refs[i], refs[count + i]
+        if src.ndim == 4 and src.shape[1] % EMIT_PARTS == 0:
+            rows = src.shape[1] // EMIT_PARTS
+            for q in range(EMIT_PARTS):
+                part = pl.ds(q * rows, rows)
+                pltpu.make_async_copy(src.at[:, part], dst.at[:, part], sem.at[i]).start()
+        else:
+            pltpu.make_async_copy(src, dst, sem.at[i]).start()
+    for i in range(count):
+        pltpu.make_async_copy(refs[i], refs[count + i], sem.at[i]).wait()
 
 
 def emit(*values):

time: 30.8 us -> 30.8 us (level)
  no operation moved by 1% of the time
where the time goes in v6:
time: 30.8 us; the launch traced here: 30.6 us
  Pallas kernels  30 us (97%)
  between operations  0.64 us (2%)
    pallas_call x1, Pallas kernels, local(): pl.pallas_call(functools.partial(kernel, nl, nd, owners, norm), out_shape...  29 us
    pallas_call x1, Pallas kernels, emit(): pl.pallas_call(emit_kernel, out_shape=[jax.ShapeDtypeStruct(v.shape, v.dt...  0.94 us

profile of v6, /device:TPU:0, one launch (start us, length us, event | category | flops | bytes accessed | tf_op | source)
XLA Modules:
  0.0 30.6 jit_solution(16218881251817374844)
XLA Ops:
  0.6 29.0 %conv_backward.1 = (bf16[1,32,48,256]{3,2,1,0:T(8,128)(2,1)S(1)}, f32[144,128]{1,0:T(8,128)S(1)}, f32[144,128]{1,0:T(8,128)S(1)}) custom-call(bf16[1,32,48,256]{3,2,1,0:T(8,128)(2,1)} %refs_0_.1, bf16[1,32,48,256]{3,2,1,0:T(8,128)(2,1)} %refs_1_.1, bf16[1,32,48,256]{3,2,1,0:T(8,128)(2,1)} %refs_2_.1, bf16[2304,256]{1,0:T(8,128)(2,1)} %refs_3_.1, ...), custom_call_target="tpu_custom_call" | custom-call | tf_op jit(solution)/shard_map/conv_backward/pallas_call | solution.py:726
  29.7 0.9 %emit.1 = (bf16[1,32,48,256]{3,2,1,0:T(8,128)(2,1)}, f32[144,128]{1,0:T(8,128)}, f32[144,128]{1,0:T(8,128)}) custom-call(bf16[1,32,48,256]{3,2,1,0:T(8,128)(2,1)S(1)} %get-tuple-element.9.refs_0_, f32[144,128]{1,0:T(8,128)S(1)} %get-tuple-element.10.refs_1_, f32[144,128]{1,0:T(8,128)S(1)} %get-tuple-element.11.refs_2_), custom_call_target="tpu_custom_call" | custom-call | tf_op jit(solution)/shard_map/emit/pallas_call | solution.py:678
